TPU v7x, 256 devices: a whole 4x4x8 slice. The times are simulated.
256 devices in a mesh: layer: 128 (over y_lo, x, z, core), src: 2 (over y_hi).
Axes of the slice: x: 4, y: 4 (y_hi: 2, y_lo: 2; y = y_hi * 2 + y_lo), z: 8, core: 2. Of those that a mesh axis runs over, the one named last changes fastest.
Arguments:
- down_maps: bfloat16 [128, 1664, 1664], P('layer'), may hold values from -1 to 1
- up_maps: bfloat16 [128, 1664, 1664], P('layer'), may hold values from -1 to 1
- local_traces: bfloat16 [128, 1664], P('src'), may hold values from -6 to 6
- src_depth: int32 [128], P('src'), may hold values from 0 to 127
Outputs:
- traces: bfloat16 [128, 128, 1664], P('layer', 'src')
- residual: bfloat16 [128, 128, 1664], P('layer', 'src')
All inputs are finite; a program needn't handle non-finite values.
Results may differ from a plain program's by a relative error of at most 0.035.
Values may be sent and summed in bfloat16 or wider, within the bound.
No kernel may reach another device: no remote copies, remote signals or barrier semaphores. Data moves between devices by JAX's collectives and lax.ppermute only.
A program may use at most 64 MiB of HBM per device.

v0:
```python
import jax
import jax.numpy as jnp
from jax import lax
from jax.sharding import PartitionSpec as P


def shifted(shard, axis, by):
    count = lax.axis_size(axis)
    pairs = [(i, i + by) for i in range(count) if 0 <= i + by < count]
    return lax.ppermute(shard, axis, pairs)


def padded_2(cells, sides, width):
    for axis, dim in sides:
        count = lax.axis_size(axis)
        ends = count - 1
        head = lax.slice_in_dim(cells, 0, width, axis=dim)
        tail = lax.slice_in_dim(cells, cells.shape[dim] - width, cells.shape[dim], axis=dim)
        cells = jnp.concatenate(
            [
                lax.ppermute(tail, axis, [(i, (i + 1) % count) for i in range(ends)]),
                cells,
                lax.ppermute(head, axis, [((i + 1) % count, i) for i in range(ends)]),
            ],
            axis=dim,
        )
    return cells


def apply_stack(maps, forcing_block, entering, layer_order):
    results = [None] * maps.shape[0]
    current = entering
    for position in layer_order:
        fresh = forcing_block[position] + jnp.dot(
            current, maps[position], preferred_element_type=jnp.float32
        )
        results[position] = fresh
        current = fresh.astype(jnp.bfloat16)
    return (jnp.stack(results), current)


def advance(maps, forcing, stored, arrived, step_index, lag, block_rows, batch_count, layer_order):
    batch_index = step_index - lag
    active = jnp.logical_and(batch_index >= 0, batch_index < batch_count)
    row_start = jnp.clip(batch_index, 0, batch_count - 1) * block_rows
    forcing_block = lax.dynamic_slice_in_dim(forcing, row_start, block_rows, 1)

    def compute_block():
        return apply_stack(maps, forcing_block, arrived, layer_order)

    def skip_block():
        return (jnp.zeros(forcing_block.shape, jnp.float32), jnp.zeros(arrived.shape, jnp.bfloat16))

    new_block, leaving = lax.cond(active, compute_block, skip_block)
    previous = lax.dynamic_slice_in_dim(stored, row_start, block_rows, 1)
    stored = lax.dynamic_update_slice_in_dim(
        stored, jnp.where(active, new_block, previous), row_start, 1
    )
    return (stored, leaving)


def shards(down_maps, up_maps, local_traces, src_depth):
    depth_count = down_maps.shape[0]
    source_rows, trace_width = local_traces.shape
    chain_len = lax.axis_size("layer")
    my_index = lax.axis_index("layer")
    layer_ids = my_index * depth_count + jnp.arange(depth_count, dtype=jnp.int32)
    placed = src_depth[None, :] == layer_ids[:, None]
    forcing = jnp.where(
        placed[:, :, None], local_traces.astype(jnp.float32)[None], jnp.float32(0.0)
    )
    block_rows = source_rows // 8
    batch_count = source_rows // block_rows
    turn_count = chain_len + batch_count - 1
    downward_order = list(range(depth_count))
    upward_order = downward_order[::-1]
    empty_store = jnp.zeros(forcing.shape, jnp.float32)
    empty_edge = jnp.zeros((block_rows, trace_width), jnp.bfloat16)
    up_lag = chain_len - 1 - my_index

    def joint_turn(step_index, state_tuple):
        down_store, down_edge, up_store, up_edge = state_tuple
        down_store, down_out = advance(
            down_maps,
            forcing,
            down_store,
            down_edge,
            step_index,
            my_index,
            block_rows,
            batch_count,
            downward_order,
        )
        up_store, up_out = advance(
            up_maps,
            forcing,
            up_store,
            up_edge,
            step_index,
            up_lag,
            block_rows,
            batch_count,
            upward_order,
        )
        down_edge = shifted(down_out, "layer", 1)
        up_edge = shifted(up_out, "layer", -1)
        return (down_store, down_edge, up_store, up_edge)

    down_store, _, up_store, _ = lax.fori_loop(
        0, turn_count, joint_turn, (empty_store, empty_edge, empty_store, empty_edge)
    )
    combined = down_store + up_store - forcing
    rounded = combined.astype(jnp.bfloat16)
    padded = padded_2(rounded, (("layer", 0),), 1)
    from_above = jnp.einsum(
        "lsw,lwv->lsv", padded[:-2], down_maps, preferred_element_type=jnp.float32
    )
    from_below = jnp.einsum("lsw,lwv->lsv", padded[2:], up_maps, preferred_element_type=jnp.float32)
    remainder = forcing - combined + from_above + from_below
    return (rounded, remainder.astype(jnp.bfloat16))


def solution(mesh):
    placed = (P("layer", None, None), P("layer", None, None), P("src", None), P("src"))
    return jax.shard_map(
        shards,
        mesh=mesh,
        in_specs=placed,
        out_specs=(P("layer", "src", None), P("layer", "src", None)),
        check_vma=False,
    )
```

profile of v0, /device:TPU:24, one launch (start us, length us, event | category | flops | bytes accessed | tf_op | source)
XLA Modules:
  0.0 1622.6 jit_solution(929725811856651731)
XLA Ops:
  2.4 1598.7 %while.19 = (s32[]{:T(128)}, f32[1,64,1664]{2,1,0:T(8,128)S(1)}, bf16[8,1664]{1,0:T(8,128)(2,1)S(1)}, f32[1,64,1664]{2,1,0:T(8,128)S(1)}, bf16[8,1664]{1,0:T(8,1...) while((s32[]{:T(128)}, f32[1,64,1664]{2,1,0:T(8,128)S(1)}, ...), condition=%wide.region_5.6_spmd, body=%wide.region_0.5_spmd.sunk | while | flops 88684560 | bytes 11928103 | solution.py:109
  4.6 9.6 collective-permute-start.1
  17.8 7.9 collective-permute-start.1
  29.2 7.9 collective-permute-start.1
  52.0 7.9 collective-permute-start.1
  63.4 7.9 collective-permute-start.1
  74.8 7.9 collective-permute-start.1
  86.2 7.9 collective-permute-start.1
  97.6 7.9 collective-permute-start.1
  109.0 7.9 collective-permute-start.1
  120.4 7.9 collective-permute-start.1
  131.8 7.9 collective-permute-start.1
  143.2 7.9 collective-permute-start.1
  154.6 7.9 collective-permute-start.1
  166.0 7.9 collective-permute-start.1
  177.4 7.9 collective-permute-start.1
  188.8 7.9 collective-permute-start.1
  200.2 7.9 collective-permute-start.1
  211.6 7.9 collective-permute-start.1
  223.0 7.9 collective-permute-start.1
  234.4 7.9 collective-permute-start.1
  245.8 7.9 collective-permute-start.1
  268.6 7.9 collective-permute-start.1
  280.0 7.9 collective-permute-start.1
  291.4 7.9 collective-permute-start.1
  302.8 7.9 collective-permute-start.1
  314.2 7.9 collective-permute-start.1
  325.6 7.9 collective-permute-start.1
  337.0 7.9 collective-permute-start.1
  348.4 7.9 collective-permute-start.1
  359.8 7.9 collective-permute-start.1
  371.2 7.9 collective-permute-start.1
  382.6 7.9 collective-permute-start.1
  394.0 7.9 collective-permute-start.1
  405.4 7.9 collective-permute-start.1
  416.8 7.9 collective-permute-start.1
  428.2 7.9 collective-permute-start.1
  439.6 7.9 collective-permute-start.1
  451.0 7.9 collective-permute-start.1
  462.4 7.9 collective-permute-start.1
  485.2 7.9 collective-permute-start.1
  496.6 7.9 collective-permute-start.1
  508.1 7.9 collective-permute-start.1
  519.5 7.9 collective-permute-start.1
  530.9 7.9 collective-permute-start.1
  542.3 7.9 collective-permute-start.1
  553.7 7.9 collective-permute-start.1
  565.1 7.9 collective-permute-start.1
  576.5 7.9 collective-permute-start.1
  587.9 7.9 collective-permute-start.1
  599.3 7.9 collective-permute-start.1
  610.7 7.9 collective-permute-start.1
  622.1 7.9 collective-permute-start.1
  633.5 7.9 collective-permute-start.1
  728.1 7.9 collective-permute-start.1
  746.2 7.9 collective-permute-start.1
  764.4 7.9 collective-permute-start.1
  782.6 7.9 collective-permute-start.1
  800.7 7.9 collective-permute-start.1
  818.9 7.9 collective-permute-start.1
  837.0 7.9 collective-permute-start.1
  855.2 7.9 collective-permute-start.1
  870.0 11.2 collective-permute-start.1
  1601.2 8.1 collective-permute-start.3
  (1425 shorter events, 1169.0 us)
Async XLA Ops:
  2.5 11.7 collective-permute-start
  4.6 11.1 collective-permute-start.1
  15.8 9.9 collective-permute-start
  27.2 9.9 collective-permute-start
  38.6 9.9 collective-permute-start
  50.0 9.9 collective-permute-start
  61.4 9.9 collective-permute-start
  72.8 9.9 collective-permute-start
  84.2 9.9 collective-permute-start
  95.6 9.9 collective-permute-start
  107.0 9.9 collective-permute-start
  118.4 9.9 collective-permute-start
  129.8 9.9 collective-permute-start
  141.2 9.9 collective-permute-start
  152.6 9.9 collective-permute-start
  164.0 9.9 collective-permute-start
  175.4 9.9 collective-permute-start
  186.8 9.9 collective-permute-start
  232.4 9.9 collective-permute-start
  266.6 9.9 collective-permute-start
  278.0 9.9 collective-permute-start
  312.2 9.9 collective-permute-start
  357.8 9.9 collective-permute-start
  403.4 9.9 collective-permute-start
  449.0 9.9 collective-permute-start
  483.3 9.9 collective-permute-start
  494.7 9.9 collective-permute-start
  528.9 9.9 collective-permute-start
  574.5 9.9 collective-permute-start
  620.1 9.9 collective-permute-start
  665.7 9.9 collective-permute-start
  699.9 9.9 collective-permute-start
  711.3 9.9 collective-permute-start
  722.7 13.3 collective-permute-start
  740.9 13.3 collective-permute-start
  759.0 13.3 collective-permute-start
  777.2 13.3 collective-permute-start
  795.3 13.3 collective-permute-start
  813.5 13.3 collective-permute-start
  831.7 13.3 collective-permute-start
  849.8 13.3 collective-permute-start
  868.0 13.3 collective-permute-start
  870.0 12.8 collective-permute-start.1
  917.0 9.9 collective-permute-start
  962.6 9.9 collective-permute-start
  1008.2 9.9 collective-permute-start
  1042.4 9.9 collective-permute-start
  1053.8 9.9 collective-permute-start
  1088.0 9.9 collective-permute-start
  1133.6 9.9 collective-permute-start
  1179.2 9.9 collective-permute-start
  1224.8 9.9 collective-permute-start
  1259.1 9.9 collective-permute-start
  1270.5 9.9 collective-permute-start
  1304.7 9.9 collective-permute-start
  1350.3 9.9 collective-permute-start
  1395.9 9.9 collective-permute-start
  1441.5 9.9 collective-permute-start
  1475.7 9.9 collective-permute-start
  1487.1 9.9 collective-permute-start
  1521.3 9.9 collective-permute-start
  1566.9 9.9 collective-permute-start
  1601.2 11.5 collective-permute-start.3
  1609.4 11.4 collective-permute-start.2
  (211 other events, 3630.8 us)
where the time goes:
time: 1640 us; the launch traced here: 1620 us
  starting transfers between devices  1340 us (82%)
  waiting for transfers between devices  205 us (12%)
  matrix products  59.9 us (4%)
    ppermute x270, starting transfers between devices, shifted(): return lax.ppermute(shard, axis, pairs)  1330 us
    ppermute x270, waiting for transfers between devices, shifted(): return lax.ppermute(shard, axis, pairs)  199 us
    dot_general x16, matrix products, apply_stack(): jnp.dot(current, maps[position], preferred_element_type=jnp.float32)  54.4 us
  transfers between devices with their start and end apart: 272, of which 137 were waited for; matrix products, arithmetic and copies ran while one was open for 2% of the time, Pallas kernels for 0%

commit v1 on v0

v1 whole, which is shorter than its diff:
```python
import jax
import jax.numpy as jnp
from jax import lax
from jax.experimental import pallas as pl
from jax.experimental.pallas import tpu as pltpu
from jax.sharding import PartitionSpec as P

BF = jnp.bfloat16
F32 = jnp.float32
SINGLES = 12
PAIRS = 32
VMEM = pl.BlockSpec(memory_space=pltpu.VMEM)
SMEM = pl.BlockSpec(memory_space=pltpu.SMEM)
HBM = pl.BlockSpec(memory_space=pl.ANY)


def limit(mib):
    return pltpu.CompilerParams(vmem_limit_bytes=mib * 2**20)


def dot(a, b):
    return jnp.dot(a, b, preferred_element_type=F32)


def by_block(extent, block, body):
    whole = extent // block

    def step(i, carry):
        body(pl.multiple_of(i * block, block), block)
        return carry

    lax.fori_loop(0, whole, step, 0)
    if extent % block:
        body(whole * block, extent % block)


def pick(meta, down, up):
    def kernel(meta_ref, down_ref, up_ref, send_ref, own_ref, sems):
        def copies(first, second):
            one = pltpu.make_async_copy(first, send_ref, sems.at[0])
            two = pltpu.make_async_copy(second, own_ref, sems.at[1])
            one.start()
            two.start()
            one.wait()
            two.wait()

        @pl.when(meta_ref[2] == 0)
        def _():
            copies(down_ref, up_ref)

        @pl.when(meta_ref[2] != 0)
        def _():
            copies(up_ref, down_ref)

    shape = jax.ShapeDtypeStruct(down.shape, BF)
    return pl.pallas_call(
        kernel,
        out_shape=(shape, shape),
        in_specs=[SMEM, HBM, HBM],
        out_specs=(VMEM, VMEM),
        scratch_shapes=[pltpu.SemaphoreType.DMA((2,))],
        compiler_params=limit(14),
        name="pick",
    )(meta, down, up)


def product(meta, least, left, tail, right, right_tail, name):
    width = right.shape[1]
    rows = right_tail.shape[0] if right_tail is not None else right.shape[0] - width
    own_tail = tail is not None

    def kernel(meta_ref, *refs):
        refs = list(refs)
        out_ref = refs.pop()
        left_ref = refs.pop(0)
        tail_ref = refs.pop(0) if own_tail else None
        right_ref = refs.pop(0)
        add_ref = refs.pop(0) if right_tail is not None else None

        @pl.when(meta_ref[0] >= least)
        def _():
            def body(start, size):
                part = dot(left_ref[pl.ds(start, size), :], right_ref[0:width, :])
                out_ref[pl.ds(start, size), :] = part.astype(BF)

            by_block(width, 256, body)
            low = tail_ref[...] if own_tail else left_ref[width:, :]
            add = add_ref[...] if add_ref is not None else right_ref[width:, :]
            out_ref[width:, :] = (dot(low, right_ref[0:width, :]) + add.astype(F32)).astype(BF)

    args = [left] + ([tail] if own_tail else []) + [right] + ([right_tail] if right_tail is not None else [])
    return pl.pallas_call(
        kernel,
        out_shape=jax.ShapeDtypeStruct((width + rows, width), BF),
        in_specs=[SMEM] + [VMEM] * len(args),
        out_specs=VMEM,
        compiler_params=limit(24),
        name=name,
    )(meta, *args)


def advance(meta, position, arrived, maps, kept, out):
    rows, width = out.shape

    def kernel(meta_ref, x_ref, maps_ref, kept_in, out_in, kept_ref, out_ref):
        @pl.when(meta_ref[0] == position)
        def _():
            x = x_ref[...]
            kept_ref[...] = x

            def body(start, size):
                cols = pl.ds(start, size)
                part = dot(x, maps_ref[0:width, cols]) + maps_ref[width:, cols].astype(F32)
                out_ref[:, cols] = part.astype(BF)

            by_block(width, 256, body)

        @pl.when(meta_ref[0] != position)
        def _():
            kept_ref[...] = kept_in[...]
            out_ref[...] = out_in[...]

    shape = jax.ShapeDtypeStruct((rows, width), BF)
    return pl.pallas_call(
        kernel,
        out_shape=(shape, shape),
        in_specs=[SMEM] + [VMEM] * 4,
        out_specs=(VMEM, VMEM),
        compiler_params=limit(9),
        name="advance",
    )(meta, arrived, maps, kept, out)


def two_layers(x, maps1_ref, maps2_ref, add1_ref, add2_ref, first_ref, second_ref, leaving_ref, mid_ref):
    width = maps1_ref.shape[1]

    def body1(start, size):
        cols = pl.ds(start, size)
        part = dot(x, maps1_ref[:, cols]) + add1_ref[:, cols].astype(F32)
        first_ref[:, cols] = part
        mid_ref[:, cols] = part.astype(BF)

    by_block(width, 256, body1)
    mid = mid_ref[...]

    def body2(start, size):
        cols = pl.ds(start, size)
        part = dot(mid, maps2_ref[:, cols]) + add2_ref[:, cols].astype(F32)
        second_ref[:, cols] = part
        leaving_ref[:, cols] = part.astype(BF)

    by_block(width, 256, body2)


def settle_first(meta, kept, entering, entering_far, maps1, maps2, add1, add2, pair_maps):
    rows, width = kept.shape

    def kernel(meta_ref, kept_ref, near_ref, far_ref, m1, m2, a1, a2, pair_ref, first, second, leaving, mid):
        role = meta_ref[1]

        @pl.when(role == 0)
        def _():
            two_layers(kept_ref[...], m1, m2, a1, a2, first, second, leaving, mid)

        @pl.when(role == 1)
        def _():
            two_layers(near_ref[...], m1, m2, a1, a2, first, second, leaving, mid)

        @pl.when((role == 2) & (meta_ref[0] >= PAIRS))
        def _():
            x = far_ref[...]

            def body(start, size):
                cols = pl.ds(start, size)
                part = dot(x, pair_ref[0:width, cols]) + pair_ref[width:, cols].astype(F32)
                leaving[:, cols] = part.astype(BF)

            by_block(width, 256, body)

    return pl.pallas_call(
        kernel,
        out_shape=(
            jax.ShapeDtypeStruct((rows, width), F32),
            jax.ShapeDtypeStruct((rows, width), F32),
            jax.ShapeDtypeStruct((rows, width), BF),
        ),
        in_specs=[SMEM] + [VMEM] * 8,
        out_specs=(VMEM, VMEM, VMEM),
        scratch_shapes=[pltpu.VMEM((rows, width), BF)],
        compiler_params=limit(24),
        name="settle_first",
    )(meta, kept, entering, entering_far, maps1, maps2, add1, add2, pair_maps)


def settle(meta, roles, entering, maps1, maps2, add1, add2, first, second):
    rows, width = entering.shape

    def kernel(meta_ref, x_ref, m1, m2, a1, a2, first_in, second_in, first_ref, second_ref, leaving, mid):
        role = meta_ref[1]

        @pl.when((role >= roles[0]) & (role <= roles[1]))
        def _():
            two_layers(x_ref[...], m1, m2, a1, a2, first_ref, second_ref, leaving, mid)

        @pl.when((role < roles[0]) | (role > roles[1]))
        def _():
            first_ref[...] = first_in[...]
            second_ref[...] = second_in[...]

    return pl.pallas_call(
        kernel,
        out_shape=(
            jax.ShapeDtypeStruct((rows, width), F32),
            jax.ShapeDtypeStruct((rows, width), F32),
            jax.ShapeDtypeStruct((rows, width), BF),
        ),
        in_specs=[SMEM] + [VMEM] * 7,
        out_specs=(VMEM, VMEM, VMEM),
        scratch_shapes=[pltpu.VMEM((rows, width), BF)],
        compiler_params=limit(18),
        name="settle",
    )(meta, entering, maps1, maps2, add1, add2, first, second)


def finish(combined, own_add, partner, outer, maps_partner, maps_outer):
    rows, width = combined.shape

    def kernel(c_ref, a_ref, x_ref, o_ref, m1, m2, out_ref):
        x = x_ref[...]
        o = o_ref[...]

        def body(start, size):
            cols = pl.ds(start, size)
            part = dot(x, m1[:, cols]) + dot(o, m2[:, cols])
            out_ref[:, cols] = (a_ref[:, cols].astype(F32) - c_ref[:, cols] + part).astype(BF)

        by_block(width, 256, body)

    return pl.pallas_call(
        kernel,
        out_shape=jax.ShapeDtypeStruct((rows, width), BF),
        in_specs=[VMEM] * 6,
        out_specs=VMEM,
        compiler_params=limit(18),
        name="finish",
    )(combined, own_add, partner, outer, maps_partner, maps_outer)


def shards(down_maps, up_maps, local_traces, src_depth):
    down, up = down_maps[0], up_maps[0]
    rows, width = local_traces.shape
    count = lax.axis_size("layer")
    chips = count // 2
    layer = lax.axis_index("layer")
    core = layer % 2
    chip = layer // 2
    position = jnp.where(core == 1, chip, chips - 1 - chip)
    role = jnp.where(
        position < SINGLES,
        0,
        jnp.where(position < PAIRS, 1 + (position - SINGLES) % 2, 1 + (position - PAIRS) % 4),
    )
    meta = jnp.stack([position, role, core]).astype(jnp.int32)

    def device(at):
        return (2 * at + 1, 2 * (chips - 1 - at))

    def links(steps):
        return [pair for a, b in steps for pair in zip(device(a), device(b))]

    def move(value, steps):
        return lax.ppermute(value, "layer", links(steps))

    partners = [(i, i ^ 1) for i in range(count)]
    zero = jnp.zeros((), BF)
    add2 = jnp.where((src_depth == layer)[:, None], local_traces, zero)
    add1 = jnp.where((src_depth == layer + 1 - 2 * core)[:, None], local_traces, zero)

    given, maps2 = pick(meta, down, up)
    maps1 = lax.ppermute(given, "layer", partners)
    one = product(meta, 0, maps1, add1, maps2, add2, "chip_product")
    evens = range(SINGLES, chips, 2)
    two = product(meta, SINGLES, move(one, [(e, e + 1) for e in evens]), None, one, None, "pair_product")
    quads = range(PAIRS, chips, 4)
    four = product(meta, PAIRS, move(two, [(e + 1, e + 3) for e in quads]), None, two, None, "quad_product")

    stops = [(at, one) for at in range(SINGLES)]
    stops += [(e + 1, two) for e in range(SINGLES, PAIRS, 2)]
    stops += [(e + 3, four) for e in range(PAIRS, chips - 4, 4)]
    blank = jnp.zeros((rows, width), BF)
    arrived, kept, out = blank, blank, blank
    last = None
    for at, maps in stops:
        if last is not None:
            arrived = move(out, [(last, at)])
        kept, out = advance(meta, at, arrived, maps, kept, out)
        last = at

    firsts = list(range(SINGLES, PAIRS, 2)) + list(quads)
    near = move(out, [(e - 1, e) for e in firsts])
    far = move(out, [(e - 1, e + 1) for e in quads])
    first, second, leaving = settle_first(meta, kept, near, far, maps1, maps2, add1, add2, two)
    entering = move(leaving, [(e, e + 1) for e in firsts] + [(e + 1, e + 2) for e in quads])
    first, second, leaving = settle(meta, (2, 3), entering, maps1, maps2, add1, add2, first, second)
    entering = move(leaving, [(e + 2, e + 3) for e in quads])
    first, second, leaving = settle(meta, (4, 4), entering, maps1, maps2, add1, add2, first, second)

    combined = second + lax.ppermute(first, "layer", partners) - add2.astype(F32)
    rounded = combined.astype(BF)
    partner = lax.ppermute(rounded, "layer", partners)
    outward = [(i, i + 1) for i in range(1, count - 1, 2)]
    outer = lax.ppermute(rounded, "layer", outward + [(b, a) for a, b in outward])
    residual = finish(combined, add2, partner, outer, maps2, given)
    return (rounded[None], residual[None])


def solution(mesh):
    placed = (P("layer", None, None), P("layer", None, None), P("src", None), P("src"))
    return jax.shard_map(
        shards,
        mesh=mesh,
        in_specs=placed,
        out_specs=(P("layer", "src", None), P("layer", "src", None)),
        check_vma=False,
    )
```

time: 1640 us -> 374 us (0.23)
  the two profiles are of different devices: /device:TPU:24 before, /device:TPU:1 now
where the time goes in v1:
time: 374 us
  starting transfers between devices  285 us (76%)
  Pallas kernels  58.3 us (16%)
  waiting for transfers between devices  18.3 us (5%)
  local copies, waits for them, and re-layouts  10.1 us (3%)
    ppermute x1, starting transfers between devices, shards(): lax.ppermute(first, 'layer', partners)  255 us
    ppermute x34, starting transfers between devices, move(): return lax.ppermute(value, 'layer', links(steps))  24.4 us
    pallas_call x29, Pallas kernels, advance(): pl.pallas_call(kernel, out_shape=(shape, shape), in_specs=[SMEM] + [VMEM]...  19 us
    pallas_call x3, Pallas kernels, product(): pl.pallas_call(kernel, out_shape=jax.ShapeDtypeStruct((width + rows, widt...  16.6 us
    unnamed x18, local copies, waits for them, and re-layouts  10.1 us
    ppermute x1, waiting for transfers between devices, shards(): maps1 = lax.ppermute(given, 'layer', partners)  8.91 us
  transfers between devices with their start and end apart: 38, of which 4 were waited for; matrix products, arithmetic and copies ran while one was open for 0% of the time, Pallas kernels for 4%

profile of v1, /device:TPU:1, one launch (start us, length us, event | category | flops | bytes accessed | tf_op | source)
XLA Modules:
  0.0 373.6 jit_solution(5375026359449925773)
XLA Ops:
  0.8 2.6 copy-done.2
  3.4 2.6 copy-done.3
  5.9 3.8 %pick.1 = (bf16[1664,1664]{1,0:T(8,128)(2,1)}, bf16[1664,1664]{1,0:T(8,128)(2,1)S(1)}) custom-call(s32[3]{0:T(128)S(1)} %pad_add_fusion.meta_ref, bf16[1664,1664]{1,0:T(8,128)(2,1)S(1)} %bitcast.9, bf16[1664,1664]{1,0:T(8,128)(2,1)S(1)} %bitcast.10), custom_call_target="tpu_custom_call" | custom-call | tf_op jit(solution)/shard_map/pick/pallas_call | solution.py:56
  9.8 2.3 copy-done
  12.1 3.2 collective-permute-start
  15.4 8.9 %collective-permute-done.refs_0_.m1 = bf16[1664,1664]{1,0:T(8,128)(2,1)} collective-permute-done((bf16[1664,1664]{1,0:T(8,128)(2,1)}, bf16[1664,1664]{1,0:T(8,128)(2,1)}, u32[]{:S(2)}, u32[]{:S(2)}) %collective-permute-start) | collective-permute-done | bytes 5537824 | tf_op jit(solution)/shard_map/ppermute | solution.py:280
  24.4 2.6 copy-done.1
  26.9 15.5 %chip_product.1.maps_ref.refs_1_ = bf16[1728,1664]{1,0:T(8,128)(2,1)S(1)} custom-call(s32[3]{0:T(128)S(1)} %pad_add_fusion.meta_ref, bf16[1664,1664]{1,0:T(8,128)(2,1)} %collective-permute-done.refs_0_.m1, bf16[64,1664]{1,0:T(8,128)(2,1)S(1)} %get-tuple-element.140.refs_1_.a1, bf16[1664,1664]{1,0:T(8,128)(2,1)S(1)} %copy-done.1, ...), custom_call_target="tpu_custom_call" | custom-call | tf_op jit(solution)/shard_map/chip_product/pallas_call | solution.py:92
  42.4 1.0 collective-permute-start.13
  44.0 1.0 collective-permute-start.24
  45.1 2.5 advance.29
  47.6 1.3 collective-permute-start.1
  48.9 2.8 collective-permute-done.1.x_ref
  52.2 0.7 collective-permute-start.2
  52.9 0.6 advance.31
  53.5 0.7 collective-permute-start.3
  54.2 0.6 advance.32
  54.8 0.7 collective-permute-start.4
  56.1 0.7 collective-permute-start.5
  57.4 0.7 collective-permute-start.6
  58.7 0.7 collective-permute-start.7
  59.3 0.6 advance.36
  59.9 0.7 collective-permute-start.8
  60.6 0.8 advance.37
  61.4 0.7 collective-permute-start.9
  62.1 0.6 advance.38
  62.7 0.7 collective-permute-start.10
  64.0 0.7 collective-permute-start.11
  65.3 0.7 collective-permute-start.12
  66.5 0.7 collective-permute-start.14
  67.2 0.6 advance.42
  67.8 0.7 collective-permute-start.15
  68.5 0.6 advance.43
  69.1 0.7 collective-permute-start.16
  69.8 0.6 advance.44
  70.4 0.7 collective-permute-start.17
  71.1 0.6 advance.45
  71.7 0.7 collective-permute-start.18
  73.0 0.7 collective-permute-start.19
  74.2 0.7 collective-permute-start.20
  75.5 0.7 collective-permute-start.21
  76.2 0.6 advance.49
  76.8 0.7 collective-permute-start.22
  77.5 0.6 advance.50
  78.1 0.7 collective-permute-start.23
  79.4 0.6 advance.51
  80.0 0.7 collective-permute-start.25
  81.2 0.7 collective-permute-start.26
  82.5 0.7 collective-permute-start.27
  83.8 0.7 collective-permute-start.28
  85.1 0.8 collective-permute-start.29
  86.5 0.7 collective-permute-start.30
  87.8 0.7 collective-permute-start.32
  88.5 0.7 collective-permute-start.31
  89.2 6.7 %settle_first.1 = (f32[64,1664]{1,0:T(8,128)S(1)}, f32[64,1664]{1,0:T(8,128)S(1)}, bf16[64,1664]{1,0:T(8,128)(2,1)S(1)}) custom-call(s32[3]{0:T(128)S(1)} %pad_add_fusion.meta_ref, bf16[64,1664]{1,0:T(8,128)(2,1)S(1)} %get-tuple-element.128.kept_ref, bf16[64,1664]{1,0:T(8,128)(2,1)S(1)} %collective-permute-done.31.near_ref, ...), custom_call_target="tpu_custom_call" | custom-call | tf_op jit(solution)/shard_map/settle_first/pallas_call | solution.py:180
  95.9 0.7 collective-permute-start.33
  96.6 2.6 settle.2
  99.3 0.7 collective-permute-start.34
  100.0 3.3 settle.3
  103.3 255.4 %collective-permute-start.35 = (f32[64,1664]{1,0:T(8,128)S(1)}, f32[64,1664]{1,0:T(8,128)S(1)}, u32[]{:S(2)}, u32[]{:S(2)}) collective-permute-start(f32[64,1664]{1,0:T(8,128)S(1)} %get-tuple-element.137), channel_id=1, source_target_pairs={{0,2},{2,0},{4,6},{6,4},{8,10},{10,8},{12,14},{14,12},{16,18},{18,... | collective-permute-start | bytes 1277960 | tf_op jit(solution)/shard_map/ppermute | solution.py:308
  358.7 1.4 collective-permute-done.35
  360.2 1.9 collective-permute-start.37
  362.2 5.1 %collective-permute-done.37.o_ref = bf16[64,1664]{1,0:T(8,128)(2,1)S(1)} collective-permute-done((bf16[64,1664]{1,0:T(8,128)(2,1)S(1)}, bf16[64,1664]{1,0:T(8,128)(2,1)S(1)}, u32[]{:S(2)}, u32[]{:S(2)}) %collective-permute-start.37) | collective-permute-done | bytes 213024 | tf_op jit(solution)/shard_map/ppermute | solution.py:312
  367.4 6.2 %finish.1 = bf16[64,1664]{1,0:T(8,128)(2,1)} custom-call(f32[64,1664]{1,0:T(8,128)S(1)} %get-tuple-element.139.c_ref, bf16[64,1664]{1,0:T(8,128)(2,1)S(1)} %get-tuple-element.141.refs_3_.a2.a_ref, bf16[64,1664]{1,0:T(8,128)(2,1)S(1)} %collective-permute-done.36.x_ref, bf16[64,1664]{1,0:T(8,128)(2,1)S(1)} %collective-permute-done.37.o_ref, ...), custom_call_target="tpu_custom_call" | custom-call | tf_op jit(solution)/shard_map/finish/pallas_call | solution.py:239
  (73 shorter events, 10.9 us)
Async XLA Ops:
  0.6 14.7 %copy-start.6 = (s32[64]{0:T(128)S(1)}, s32[64]{0:T(128)}, u32[]{:S(2)}) copy-start(s32[64]{0:T(128)} %param.7) | copy-start | bytes 772
  0.8 2.6 copy-start.2
  3.4 2.6 copy-start.3
  5.9 9.4 %copy-start.4 = (bf16[64,1664]{1,0:T(8,128)(2,1)S(1)}, bf16[64,1664]{1,0:T(8,128)(2,1)}, u32[]{:S(2)}) copy-start(bf16[64,1664]{1,0:T(8,128)(2,1)} %param.6) | copy-start | bytes 638980
  9.7 2.4 copy-start
  12.1 12.3 %collective-permute-start = (bf16[1664,1664]{1,0:T(8,128)(2,1)}, bf16[1664,1664]{1,0:T(8,128)(2,1)}, u32[]{:S(2)}, u32[]{:S(2)}) collective-permute-start(bf16[1664,1664]{1,0:T(8,128)(2,1)} %get-tuple-element.70.m2), channel_id=1, source_target_pairs={{0,2},{2,0},{4,6},{6,4},{8,10},{10,8},{12,14},{14,12},{16,18},{18,... | collective-permute-start | bytes 16613384 | tf_op jit(solution)/shard_map/ppermute | solution.py:280
  24.4 2.6 copy-start.1
  42.4 1.0 collective-permute-start.13
  44.0 34.8 %collective-permute-start.24 = (bf16[1728,1664]{1,0:T(8,128)(2,1)S(1)}, bf16[1728,1664]{1,0:T(8,128)(2,1)S(1)}, u32[]{:S(2)}, u32[]{:S(2)}) collective-permute-start(bf16[1728,1664]{1,0:T(8,128)(2,1)S(1)} %pair_product.1.maps_ref.refs_1_.pair_ref), channel_id=1, source_target_pairs={{134,142},{120,112},{150,158},{104,96},{166,174},{88,80},{182,190}... | collective-permute-start | bytes 17252360 | tf_op jit(solution)/shard_map/ppermute | solution.py:272
  47.6 4.1 %collective-permute-start.1 = (bf16[64,1664]{1,0:T(8,128)(2,1)S(1)}, bf16[64,1664]{1,0:T(8,128)(2,1)S(1)}, u32[]{:S(2)}, u32[]{:S(2)}) collective-permute-start(bf16[64,1664]{1,0:T(8,128)(2,1)S(1)} %get-tuple-element.72.out_in), channel_id=1, source_target_pairs={{2,6},{252,248},{3,7},{253,249}} | collective-permute-start | bytes 638984 | tf_op jit(solution)/shard_map/ppermute | solution.py:272
  52.2 0.7 collective-permute-start.2
  53.5 0.7 collective-permute-start.3
  54.8 0.7 collective-permute-start.4
  56.1 0.7 collective-permute-start.5
  57.4 0.7 collective-permute-start.6
  58.7 0.7 collective-permute-start.7
  59.9 0.7 collective-permute-start.8
  61.4 0.7 collective-permute-start.9
  62.7 0.7 collective-permute-start.10
  64.0 0.7 collective-permute-start.11
  65.3 0.7 collective-permute-start.12
  66.5 0.7 collective-permute-start.14
  67.8 0.7 collective-permute-start.15
  69.1 0.7 collective-permute-start.16
  70.4 0.7 collective-permute-start.17
  71.7 0.7 collective-permute-start.18
  73.0 0.7 collective-permute-start.19
  74.2 0.7 collective-permute-start.20
  75.5 0.7 collective-permute-start.21
  76.8 0.7 collective-permute-start.22
  78.1 1.3 collective-permute-start.23
  80.0 0.7 collective-permute-start.25
  81.2 0.7 collective-permute-start.26
  82.5 0.7 collective-permute-start.27
  83.8 0.7 collective-permute-start.28
  84.5 4.7 %slice-start = ((s8[5537792]{0:T(1024)(128)(4,1)}), s8[4194304]{0:T(1024)(128)(4,1)S(1)}, s32[]{:S(2)}) async-start(s8[5537792]{0:T(1024)(128)(4,1)} %bitcast.7), calls=%async_computation | async-start | bytes 8388608
  85.1 0.8 collective-permute-start.29
  85.9 3.3 slice-start.1
  86.5 0.7 collective-permute-start.30
  87.8 1.4 collective-permute-start.32
  88.5 0.7 collective-permute-start.31
  95.9 0.7 collective-permute-start.33
  99.3 0.7 collective-permute-start.34
  103.3 256.8 %collective-permute-start.35 = (f32[64,1664]{1,0:T(8,128)S(1)}, f32[64,1664]{1,0:T(8,128)S(1)}, u32[]{:S(2)}, u32[]{:S(2)}) collective-permute-start(f32[64,1664]{1,0:T(8,128)S(1)} %get-tuple-element.137), channel_id=1, source_target_pairs={{0,2},{2,0},{4,6},{6,4},{8,10},{10,8},{12,14},{14,12},{16,18},{18,... | collective-permute-start | bytes 1277960 | tf_op jit(solution)/shard_map/ppermute | solution.py:308
  360.2 13.4 %copy-start.5 = (bf16[64,1664]{1,0:T(8,128)(2,1)}, bf16[64,1664]{1,0:T(8,128)(2,1)S(1)}, u32[]{:S(2)}) copy-start(bf16[64,1664]{1,0:T(8,128)(2,1)S(1)} %get-tuple-element.138) | copy-start | bytes 638980
  360.2 7.2 %collective-permute-start.37 = (bf16[64,1664]{1,0:T(8,128)(2,1)S(1)}, bf16[64,1664]{1,0:T(8,128)(2,1)S(1)}, u32[]{:S(2)}, u32[]{:S(2)}) collective-permute-start(bf16[64,1664]{1,0:T(8,128)(2,1)S(1)} %get-tuple-element.138), channel_id=1, source_target_pairs={{2,4},{6,8},{10,12},{14,16},{18,20},{22,24},{26,28},{30,32},{34,36... | collective-permute-start | bytes 638984 | tf_op jit(solution)/shard_map/ppermute | solution.py:312
  362.1 5.2 %collective-permute-start.36 = (bf16[64,1664]{1,0:T(8,128)(2,1)S(1)}, bf16[64,1664]{1,0:T(8,128)(2,1)S(1)}, u32[]{:S(2)}, u32[]{:S(2)}) collective-permute-start(bf16[64,1664]{1,0:T(8,128)(2,1)S(1)} %get-tuple-element.138), channel_id=1, source_target_pairs={{0,2},{2,0},{4,6},{6,4},{8,10},{10,8},{12,14},{14,12},{16,18},{18,... | collective-permute-start | bytes 638984 | tf_op jit(solution)/shard_map/ppermute | solution.py:310
